TPU v7x, 128 devices: a whole 4x4x4 slice. The times are simulated.
128 devices in a mesh: beta: 64 (over z, y, x), grp: 2 (over core).
Axes of the slice: x: 4, y: 4, z: 4, core: 2. Of those that a mesh axis runs over, the one named last changes fastest.
Arguments:
- samples: float32 [128, 8, 128, 128], P('beta', 'grp'), parts along dimension 1, may hold values from -6 to 6
Outputs:
- coeffs: float32 [128, 2, 8, 64, 64], P('beta', None, 'grp'), parts along dimension 2
- power: float32 [8, 64], P('grp'), parts along dimension 0
There are 2 independent parts, one for each index of `grp`. A program takes and returns all parts, laid end to end along the dimension named above; each array names one. Nothing has to cross between parts.
All inputs are finite; a program needn't handle non-finite values.
Results may differ from a plain program's by a relative error of at most 0.0003.
Values sent between devices are 32-bit elements; how exact they have to be, the bound alone decides.
A program may use at most 64 MiB of HBM per device.

v0:
```python
import jax
import jax.numpy as jnp
from jax import lax
from jax.sharding import PartitionSpec as P

HIGHEST = lax.Precision.HIGHEST


def swapped(value, axis, apart):
    mask = 2**apart
    pairs = [(source, source ^ mask) for source in range(lax.axis_size(axis))]
    return lax.ppermute(value, axis, pairs)


def from_everyone(shard, axis):
    peers = lax.axis_size(axis)
    return lax.all_to_all(
        jnp.broadcast_to(shard[None], (peers, *shard.shape)), axis, 0, 0, tiled=True
    )


def taken_together(shard, axis):
    return from_everyone(shard, axis).sum(axis=0)


def beta_angles(spread):
    grid_size = 2 * spread
    return (2.0 * jnp.arange(grid_size, dtype=jnp.float32) + 1.0) * (jnp.pi / (4.0 * spread))


def quadrature(spread):
    angles = beta_angles(spread)
    odd_terms = 2.0 * jnp.arange(spread, dtype=jnp.float32) + 1.0
    series = jnp.sum(jnp.sin(angles[:, None] * odd_terms[None, :]) / odd_terms[None, :], axis=1)
    return 2.0 / spread * jnp.sin(angles) * series


def gamma_table(spread):
    grid_size = 2 * spread
    positions = jnp.arange(grid_size, dtype=jnp.int32)
    orders = jnp.arange(spread, dtype=jnp.int32)
    phase_index = positions[:, None] * orders[None, :] % grid_size
    angles = phase_index.astype(jnp.float32) * (2.0 * jnp.pi / grid_size)
    return jnp.concatenate([jnp.cos(angles), -jnp.sin(angles)], axis=1)


def alpha_table(spread, row_index):
    grid_size = 2 * spread
    positions = jnp.arange(grid_size, dtype=jnp.int32)
    phase_index = row_index[:, None] * positions[None, :] % grid_size
    angles = phase_index.astype(jnp.float32) * (2.0 * jnp.pi / grid_size)
    cosine = jnp.cos(angles) / grid_size
    sine_part = jnp.sin(angles) / grid_size
    real_rows = jnp.stack([cosine, sine_part], axis=1)
    imag_rows = jnp.stack([-sine_part, cosine], axis=1)
    return jnp.stack([real_rows, imag_rows], axis=0)


def log_factorial(value, float_type):
    return lax.lgamma((value + 1).astype(float_type))


def wigner_start(alpha_order, gamma_order, log_cosine, log_sine):
    float_type = log_cosine.dtype
    lowest = jnp.maximum(jnp.abs(alpha_order), gamma_order)
    shift_low = jnp.maximum(0, gamma_order - alpha_order)
    magnitude = 0.5 * (
        log_factorial(lowest + alpha_order, float_type)
        + log_factorial(lowest - alpha_order, float_type)
        + log_factorial(lowest + gamma_order, float_type)
        + log_factorial(lowest - gamma_order, float_type)
    )
    magnitude = (
        magnitude
        - log_factorial(lowest + gamma_order - shift_low, float_type)
        - log_factorial(shift_low, float_type)
    )
    magnitude = magnitude - log_factorial(alpha_order - gamma_order + shift_low, float_type)
    magnitude = magnitude - log_factorial(lowest - alpha_order - shift_low, float_type)
    cos_power = (2 * lowest + gamma_order - alpha_order - 2 * shift_low).astype(float_type)
    sin_power = (alpha_order - gamma_order + 2 * shift_low).astype(float_type)
    parity = (alpha_order - gamma_order + shift_low) % 2
    sign_factor = (1 - 2 * parity).astype(float_type)
    return sign_factor * jnp.exp(magnitude + cos_power * log_cosine + sin_power * log_sine)


def advance(degree, carried, alpha_order, gamma_order, cos_angles, start_value, lowest):
    former, current = carried
    float_type = current.dtype
    previous = (degree - 1).astype(float_type)
    alpha_float = alpha_order.astype(float_type)
    gamma_float = gamma_order.astype(float_type)
    cross_ratio = alpha_float * gamma_float / jnp.maximum(previous * (previous + 1.0), 1.0)
    upper_term = ((previous + 1.0) * (previous + 1.0) - alpha_float * alpha_float) * (
        (previous + 1.0) * (previous + 1.0) - gamma_float * gamma_float
    )
    lower_term = (previous * previous - alpha_float * alpha_float) * (
        previous * previous - gamma_float * gamma_float
    )
    root_upper = jnp.sqrt(jnp.maximum(upper_term, 1.0))
    forward = (previous + 1.0) * (2.0 * previous + 1.0) / root_upper
    backward = (
        (previous + 1.0)
        * jnp.sqrt(jnp.maximum(lower_term, 0.0))
        / (jnp.maximum(previous, 1.0) * root_upper)
    )
    recurred = forward * (cos_angles - cross_ratio) * current - backward * former
    renewed = jnp.where(degree == lowest, start_value, recurred)
    return (current, renewed)


def degree_rows(row_index, weighted, spread):
    stride = 8
    grid_size = 2 * spread
    group_size = row_index.shape[0]
    channels = weighted.shape[2]
    block_count = spread // stride
    alpha_order = jnp.where(row_index < spread, row_index, row_index - grid_size)[:, None, None]
    gamma_order = jnp.arange(spread, dtype=jnp.int32)[None, None, :]
    angles = beta_angles(spread)
    cos_angles = jnp.cos(angles)[None, :, None]
    log_cosine = jnp.log(jnp.cos(0.5 * angles))[None, :, None]
    log_sine = jnp.log(jnp.sin(0.5 * angles))[None, :, None]
    lowest = jnp.maximum(jnp.abs(alpha_order), gamma_order)
    start_value = wigner_start(alpha_order, gamma_order, log_cosine, log_sine)
    first_block = jnp.min(jnp.abs(alpha_order)) // stride
    empty_state = jnp.zeros((group_size, grid_size, spread), jnp.float32)

    def compute_block(operands):
        block_index, former, current = operands
        levels = []
        for offset in range(stride):
            former, current = advance(
                block_index * stride + offset,
                (former, current),
                alpha_order,
                gamma_order,
                cos_angles,
                start_value,
                lowest,
            )
            levels.append(current)
        stacked = jnp.stack(levels, axis=0)
        block_part = jnp.einsum("jgkq,kgcq->gcjq", stacked, weighted, precision=HIGHEST)
        return (former, current, block_part)

    def skip_block(operands):
        block_index, former, current = operands
        return (former, current, jnp.zeros((group_size, channels, stride, spread), jnp.float32))

    def block_step(carried, block_index):
        former, current = carried
        former, current, block_part = lax.cond(
            block_index >= first_block, compute_block, skip_block, (block_index, former, current)
        )
        return ((former, current), block_part)

    _, parts = lax.scan(
        block_step, (empty_state, empty_state), jnp.arange(block_count, dtype=jnp.int32)
    )
    output = jnp.transpose(parts, (1, 2, 0, 3, 4)).reshape(group_size, channels, spread, spread)
    degree_scale = 8.0 * jnp.sqrt(2.0 * jnp.arange(spread, dtype=jnp.float32) + 1.0)
    return output * degree_scale[None, None, :, None]


def degree_energy(coeffs, functions, spread):
    split_view = coeffs.reshape(coeffs.shape[0], 2, functions, spread, spread)
    multiplicity = jnp.where(jnp.arange(spread) == 0, 1.0, 2.0).astype(jnp.float32)
    energy_sum = jnp.sum(split_view * split_view * multiplicity, axis=(0, 1, 4))
    degrees = 2.0 * jnp.arange(spread, dtype=jnp.float32) + 1.0
    return energy_sum / (degrees * degrees)[None, :]


def local(samples):
    devices = lax.axis_size("beta")
    device = lax.axis_index("beta")
    local_beta = samples.shape[0]
    functions = samples.shape[1]
    grid_size = samples.shape[2]
    spread = grid_size // 2
    channels = 2 * functions
    row_count = grid_size // devices
    natural_rows = jnp.arange(grid_size, dtype=jnp.int32)
    folded = natural_rows.reshape(2, devices // 2, row_count // 2, 2)
    row_order = jnp.stack([folded[:, :, :, 0], folded[::-1, :, :, 1]], axis=3).reshape(grid_size)
    halfway = jnp.einsum("kfag,gx->kfax", samples, gamma_table(spread), precision=HIGHEST)
    halfway = halfway.reshape(local_beta, functions, grid_size, 2, spread)
    spectrum = jnp.einsum(
        "kfacq,spca->kpsfq", halfway, alpha_table(spread, row_order), precision=HIGHEST
    )
    spectrum = spectrum.reshape(local_beta, grid_size, channels, spread)
    received = lax.all_to_all(spectrum, "beta", split_axis=1, concat_axis=0, tiled=True)
    weighted = received * quadrature(spread)[:, None, None, None]
    owned_rows = lax.dynamic_slice_in_dim(row_order, device * row_count, row_count)
    computed = degree_rows(owned_rows, weighted, spread)
    power_part = degree_energy(computed, functions, spread)
    kept = computed[0::2]
    lent = computed[1::2]
    returned = swapped(lent, "beta", devices.bit_length() - 2)
    coeffs = jnp.stack([kept, returned], axis=1).reshape(row_count, channels, spread, spread)
    power = taken_together(power_part, "beta")
    coeffs = coeffs.reshape(row_count, 2, functions, spread, spread)
    return (coeffs, power)


def solution(mesh):
    return jax.shard_map(
        local,
        mesh=mesh,
        in_specs=(P("beta", "grp", None, None),),
        out_specs=(P("beta", None, "grp", None, None), P("grp", None)),
        check_vma=False,
    )
```

profile of v0, /device:TPU:0, one launch (start us, length us, event | category | flops | bytes accessed | tf_op | source)
XLA Modules:
  0.0 99.0 jit_solution(18264558040937235246)
XLA Ops:
  1.1 0.3 sine_multiply_fusion
  1.5 0.2 copy-done
  1.7 0.6 fusion.30
  2.3 0.6 convolution_bitcast_fusion.1
  2.9 0.5 copy.59
  3.5 1.4 %reshape.2616 = f32[64,1,2048]{2,1,0:T(1,128)} reshape(f32[128,2,8,64]{3,2,1,0:T(8,128)S(1)} %bitcast.243) | data formatting | bytes 1048576
  4.9 11.5 %all-to-all-start = ((f32[64,1,2048]{2,1,0:T(1,128)}), f32[64,1,2048]{2,1,0:T(1,128)S(1)}, u32[]{:S(2)}, u32[]{:S(2)}) async-start(f32[64,1,2048]{2,1,0:T(1,128)} %reshape.2616), calls=%async_computation | async-start | bytes 1048576 | tf_op jit(solution)/shard_map/all_to_all | solution.py:192
  16.5 0.7 abs_reduce_fusion
  20.2 0.3 fusion.58
  20.5 9.3 %all-to-all-done = f32[64,1,2048]{2,1,0:T(1,128)S(1)} async-done(((f32[64,1,2048]{2,1,0:T(1,128)}), f32[64,1,2048]{2,1,0:T(1,128)S(1)}, u32[]{:S(2)}, u32[]{:S(2)}) %all-to-all-start) | async-done | bytes 524320 | tf_op jit(solution)/shard_map/all_to_all | solution.py:192
  29.8 0.5 broadcast.2750
  30.3 1.9 %reduce.3 = f32[64,2048]{1,0:T(8,128)S(1)} reduce(f32[64,1,2048]{2,1,0:T(1,128)S(1)} %all-to-all-done, f32[]{:T(128)} %broadcast.2750), dimensions={1}, to_apply=%all_to_all.16.reduce_sub_computation | reduce | bytes 1048580 | tf_op jit(solution)/shard_map/all_to_all | solution.py:192
  32.2 0.4 reshape.2617
  32.9 0.5 copy.62
  33.4 46.3 %while.16 = (s32[]{:T(128)}, f32[2,128,64]{1,2,0:T(8,128)S(1)}, f32[2,128,64]{1,2,0:T(8,128)S(1)}, f32[8,2,8,8,64]{4,3,0,2,1:T(8,128)S(1)}, s32[8]{0:T(128)S(1)}...) while((s32[]{:T(128)}, f32[2,128,64]{1,2,0:T(8,128)S(1)}, ...), condition=%wide.region_5.6_spmd.clone.clone, body=%wide.region_2.5_spmd.clone.clone.sunk | while | flops 13465411 | bytes 3031079 | solution.py:158
  33.5 0.6 dynamic_slice.13
  34.6 4.4 %conditional.4 = (f32[2,128,64]{1,2,0:T(8,128)S(1)}, f32[2,128,64]{1,2,0:T(8,128)S(1)}, f32[1,2,8,8,64]{2,3,4,1,0:T(8,128)S(1)}) conditional(s32[]{:T(128)} %convert_element_type.314, (f32[2,128,64]{1,2,0:T(8,128)S(1)}, f32[2,128,64]{1,2,0:T(8,128)S(1)}) %tuple.142, (s32[]{:T(128)}, s32[2]{0:T(128)S(1)}, s32[2,1,1]{0,2,1:T(1,128)S(1)}, ...), branch_computations={%region_3.3_spmd, %region_4.4_spmd.clone} | conditional | flops 13465407 | bytes 2832748 | solution.py:153
  36.4 0.8 fusion.11
  37.2 0.8 stack.67
  38.0 1.0 convolution_bitcast_fusion
  39.0 0.2 copy.77
  39.2 0.6 dynamic_slice.13
  40.4 4.4 %conditional.4 = (f32[2,128,64]{1,2,0:T(8,128)S(1)}, f32[2,128,64]{1,2,0:T(8,128)S(1)}, f32[1,2,8,8,64]{2,3,4,1,0:T(8,128)S(1)}) conditional(s32[]{:T(128)} %convert_element_type.314, (f32[2,128,64]{1,2,0:T(8,128)S(1)}, f32[2,128,64]{1,2,0:T(8,128)S(1)}) %tuple.142, (s32[]{:T(128)}, s32[2]{0:T(128)S(1)}, s32[2,1,1]{0,2,1:T(1,128)S(1)}, ...), branch_computations={%region_3.3_spmd, %region_4.4_spmd.clone} | conditional | flops 13465407 | bytes 2832748 | solution.py:153
  42.2 0.8 fusion.11
  43.0 0.8 stack.67
  43.8 1.0 convolution_bitcast_fusion
  44.8 0.2 copy.77
  45.0 0.6 dynamic_slice.13
  46.2 4.4 %conditional.4 = (f32[2,128,64]{1,2,0:T(8,128)S(1)}, f32[2,128,64]{1,2,0:T(8,128)S(1)}, f32[1,2,8,8,64]{2,3,4,1,0:T(8,128)S(1)}) conditional(s32[]{:T(128)} %convert_element_type.314, (f32[2,128,64]{1,2,0:T(8,128)S(1)}, f32[2,128,64]{1,2,0:T(8,128)S(1)}) %tuple.142, (s32[]{:T(128)}, s32[2]{0:T(128)S(1)}, s32[2,1,1]{0,2,1:T(1,128)S(1)}, ...), branch_computations={%region_3.3_spmd, %region_4.4_spmd.clone} | conditional | flops 13465407 | bytes 2832748 | solution.py:153
  48.0 0.8 fusion.11
  48.8 0.8 stack.67
  49.6 1.0 convolution_bitcast_fusion
  50.8 0.6 dynamic_slice.13
  52.0 4.4 %conditional.4 = (f32[2,128,64]{1,2,0:T(8,128)S(1)}, f32[2,128,64]{1,2,0:T(8,128)S(1)}, f32[1,2,8,8,64]{2,3,4,1,0:T(8,128)S(1)}) conditional(s32[]{:T(128)} %convert_element_type.314, (f32[2,128,64]{1,2,0:T(8,128)S(1)}, f32[2,128,64]{1,2,0:T(8,128)S(1)}) %tuple.142, (s32[]{:T(128)}, s32[2]{0:T(128)S(1)}, s32[2,1,1]{0,2,1:T(1,128)S(1)}, ...), branch_computations={%region_3.3_spmd, %region_4.4_spmd.clone} | conditional | flops 13465407 | bytes 2832748 | solution.py:153
  53.8 0.8 fusion.11
  54.6 0.8 stack.67
  55.4 1.0 convolution_bitcast_fusion
  56.6 0.6 dynamic_slice.13
  57.7 4.4 %conditional.4 = (f32[2,128,64]{1,2,0:T(8,128)S(1)}, f32[2,128,64]{1,2,0:T(8,128)S(1)}, f32[1,2,8,8,64]{2,3,4,1,0:T(8,128)S(1)}) conditional(s32[]{:T(128)} %convert_element_type.314, (f32[2,128,64]{1,2,0:T(8,128)S(1)}, f32[2,128,64]{1,2,0:T(8,128)S(1)}) %tuple.142, (s32[]{:T(128)}, s32[2]{0:T(128)S(1)}, s32[2,1,1]{0,2,1:T(1,128)S(1)}, ...), branch_computations={%region_3.3_spmd, %region_4.4_spmd.clone} | conditional | flops 13465407 | bytes 2832748 | solution.py:153
  59.6 0.8 fusion.11
  60.4 0.8 stack.67
  61.2 1.0 convolution_bitcast_fusion
  62.4 0.6 dynamic_slice.13
  63.5 4.4 %conditional.4 = (f32[2,128,64]{1,2,0:T(8,128)S(1)}, f32[2,128,64]{1,2,0:T(8,128)S(1)}, f32[1,2,8,8,64]{2,3,4,1,0:T(8,128)S(1)}) conditional(s32[]{:T(128)} %convert_element_type.314, (f32[2,128,64]{1,2,0:T(8,128)S(1)}, f32[2,128,64]{1,2,0:T(8,128)S(1)}) %tuple.142, (s32[]{:T(128)}, s32[2]{0:T(128)S(1)}, s32[2,1,1]{0,2,1:T(1,128)S(1)}, ...), branch_computations={%region_3.3_spmd, %region_4.4_spmd.clone} | conditional | flops 13465407 | bytes 2832748 | solution.py:153
  65.4 0.8 fusion.11
  66.2 0.8 stack.67
  67.0 1.0 convolution_bitcast_fusion
  68.0 0.2 copy.77
  68.2 0.6 dynamic_slice.13
  69.3 4.4 %conditional.4 = (f32[2,128,64]{1,2,0:T(8,128)S(1)}, f32[2,128,64]{1,2,0:T(8,128)S(1)}, f32[1,2,8,8,64]{2,3,4,1,0:T(8,128)S(1)}) conditional(s32[]{:T(128)} %convert_element_type.314, (f32[2,128,64]{1,2,0:T(8,128)S(1)}, f32[2,128,64]{1,2,0:T(8,128)S(1)}) %tuple.142, (s32[]{:T(128)}, s32[2]{0:T(128)S(1)}, s32[2,1,1]{0,2,1:T(1,128)S(1)}, ...), branch_computations={%region_3.3_spmd, %region_4.4_spmd.clone} | conditional | flops 13465407 | bytes 2832748 | solution.py:153
  71.2 0.8 fusion.11
  71.9 0.8 stack.67
  72.8 1.0 convolution_bitcast_fusion
  74.0 0.6 dynamic_slice.13
  75.1 4.4 %conditional.4 = (f32[2,128,64]{1,2,0:T(8,128)S(1)}, f32[2,128,64]{1,2,0:T(8,128)S(1)}, f32[1,2,8,8,64]{2,3,4,1,0:T(8,128)S(1)}) conditional(s32[]{:T(128)} %convert_element_type.314, (f32[2,128,64]{1,2,0:T(8,128)S(1)}, f32[2,128,64]{1,2,0:T(8,128)S(1)}) %tuple.142, (s32[]{:T(128)}, s32[2]{0:T(128)S(1)}, s32[2,1,1]{0,2,1:T(1,128)S(1)}, ...), branch_computations={%region_3.3_spmd, %region_4.4_spmd.clone} | conditional | flops 13465407 | bytes 2832748 | solution.py:153
  77.0 0.8 fusion.11
  77.7 0.8 stack.67
  78.6 1.0 convolution_bitcast_fusion
  80.0 0.7 collective-permute-start
  80.7 0.2 fusion.24
  81.2 15.4 %all_to_all.23 = f32[64,1,256]{2,1,0:T(1,128)S(1)} all-to-all(f32[64,1,256]{2,1,0:T(1,128)S(1)} %reshape.2618), channel_id=1, replica_groups=mesh['beta'=64,'grp'=2] {'beta'}, dimensions={0} | all-to-all | bytes 131072 | tf_op jit(solution)/shard_map/all_to_all | solution.py:17
  96.6 0.8 reduce.4
  97.5 0.7 reduce_sum.38
  98.2 0.8 pad_maximum_fusion
  (257 shorter events, 10.9 us)
Async XLA Ops:
  0.6 1.0 %copy-start = (f32[2,4,128,128]{3,2,1,0:T(8,128)S(1)}, f32[2,4,128,128]{3,2,1,0:T(8,128)}, u32[]{:S(2)}) copy-start(f32[2,4,128,128]{3,2,1,0:T(8,128)} %param.5) | copy-start | bytes 1572868
  4.9 24.9 %all-to-all-start = ((f32[64,1,2048]{2,1,0:T(1,128)}), f32[64,1,2048]{2,1,0:T(1,128)S(1)}, u32[]{:S(2)}, u32[]{:S(2)}) async-start(f32[64,1,2048]{2,1,0:T(1,128)} %reshape.2616), calls=%async_computation | async-start | bytes 1048576 | tf_op jit(solution)/shard_map/all_to_all | solution.py:192
  80.0 18.2 %collective-permute-start = (f32[1,8,64,64]{3,2,1,0:T(8,128)S(1)}, f32[1,8,64,64]{3,2,1,0:T(8,128)S(1)}, u32[]{:S(2)}, u32[]{:S(2)}) collective-permute-start(f32[1,8,64,64]{3,2,1,0:T(8,128)S(1)} %get-tuple-element.575), channel_id=1, source_target_pairs={{0,64},{2,66},{4,68},{6,70},{8,72},{10,74},{12,76},{14,78},{16,80}... | collective-permute-start | bytes 393224 | tf_op jit(solution)/shard_map/ppermute | solution.py:12
where the time goes:
time: 99.5 us; the launch traced here: 99 us
  other arithmetic  20.7 us (21%)
  local copies, waits for them, and re-layouts  17.3 us (17%)
  blocking collectives  15.4 us (15%)
  starting transfers between devices  12.2 us (12%)
  loops' own time  11.7 us (12%)
  waiting for transfers between devices  9.26 us (9%)
  matrix products  8.89 us (9%)
  between operations  3.47 us (3%)
    all_to_all x1, blocking collectives, from_everyone(): lax.all_to_all(jnp.broadcast_to(shard[None], (peers, *shard.shape)), axis...  15.4 us
    all_to_all x1, starting transfers between devices, local(): lax.all_to_all(spectrum, 'beta', split_axis=1, concat_axis=0, tiled=True)  11.5 us
    all_to_all x1, waiting for transfers between devices, local(): lax.all_to_all(spectrum, 'beta', split_axis=1, concat_axis=0, tiled=True)  9.26 us
    dot_general x8, matrix products, compute_block(): jnp.einsum('jgkq,kgcq->gcjq', stacked, weighted, precision=HIGHEST)  7.68 us
    another operation x8, loops' own time, block_step(): lax.cond(block_index >= first_block, compute_block, skip_block, (block_in...  7.04 us
    another operation x8, local copies, waits for them, and re-layouts, compute_block(): stacked = jnp.stack(levels, axis=0)  6.64 us
    select_n x8, other arithmetic, advance(): renewed = jnp.where(degree == lowest, start_value, recurred)  6.16 us
    div x64, other arithmetic, advance(): forward = (previous + 1.0) * (2.0 * previous + 1.0) / root_upper  5.32 us
  transfers between devices with their start and end apart: 2, of which 1 were waited for; matrix products, arithmetic and copies ran while one was open for 4% of the time, Pallas kernels for 0%

commit v1 on v0

--- a/solution.py
+++ b/solution.py
@@ -189,7 +189,10 @@
         "kfacq,spca->kpsfq", halfway, alpha_table(spread, row_order), precision=HIGHEST
     )
     spectrum = spectrum.reshape(local_beta, grid_size, channels, spread)
-    received = lax.all_to_all(spectrum, "beta", split_axis=1, concat_axis=0, tiled=True)
+    received = jnp.concatenate(
+        lax.all_to_all(jnp.stack(jnp.split(spectrum, lax.axis_size("beta"), axis=1)), "beta", 0, 0),
+        axis=0,
+    )
     weighted = received * quadrature(spread)[:, None, None, None]
     owned_rows = lax.dynamic_slice_in_dim(row_order, device * row_count, row_count)
     computed = degree_rows(owned_rows, weighted, spread)

time: 99.5 us -> 197 us (1.98); the launches traced: 99 us -> 193 us
  local copies, waits for them, and re-layouts: 17.3 us -> 111 us
    another operation x0 -> x69, local copies, waits for them, and re-layouts: none -> 57.8 us  [local(): jnp.stack(jnp.split(spectrum, lax.axis_size('beta'), axis=1))]
    unnamed x7 -> x262, local copies, waits for them, and re-layouts: 2.82 us -> 38.7 us
  transfers between devices with their start and end apart: 2 -> 2, of which waited for: 1 -> 1; matrix products, arithmetic and copies ran while one was open for 4% -> 2% of each run, Pallas kernels for 0% -> 0%
where the time goes in v1:
time: 197 us; the launch traced here: 193 us
  local copies, waits for them, and re-layouts  111 us (56%)
  other arithmetic  20.7 us (11%)
  blocking collectives  15.4 us (8%)
  loops' own time  12.8 us (6%)
  starting transfers between devices  12.5 us (6%)
  matrix products  8.89 us (5%)
  waiting for transfers between devices  8.87 us (5%)
  between operations  3.45 us (2%)
    another operation x69, local copies, waits for them, and re-layouts, local(): jnp.stack(jnp.split(spectrum, lax.axis_size('beta'), axis=1))  57.8 us
    unnamed x262, local copies, waits for them, and re-layouts  38.7 us
    all_to_all x1, blocking collectives, from_everyone(): lax.all_to_all(jnp.broadcast_to(shard[None], (peers, *shard.shape)), axis...  15.4 us
    all_to_all x1, starting transfers between devices, local(): lax.all_to_all(jnp.stack(jnp.split(spectrum, lax.axis_size('beta'), axis=...  11.7 us
    all_to_all x1, waiting for transfers between devices, local(): lax.all_to_all(jnp.stack(jnp.split(spectrum, lax.axis_size('beta'), axis=...  8.86 us
    dot_general x8, matrix products, compute_block(): jnp.einsum('jgkq,kgcq->gcjq', stacked, weighted, precision=HIGHEST)  7.68 us
    another operation x8, loops' own time, block_step(): lax.cond(block_index >= first_block, compute_block, skip_block, (block_in...  7.59 us
    another operation x8, local copies, waits for them, and re-layouts, compute_block(): stacked = jnp.stack(levels, axis=0)  6.64 us
  transfers between devices with their start and end apart: 2, of which 1 were waited for; matrix products, arithmetic and copies ran while one was open for 2% of the time, Pallas kernels for 0%

profile of v1, /device:TPU:0, one launch (start us, length us, event | category | flops | bytes accessed | tf_op | source)
XLA Modules:
  0.0 193.3 jit_solution(17235466490859856298)
XLA Ops:
  2.9 1.8 slice_bitcast_fusion.57
  4.7 6.3 %slice_bitcast_fusion.38 = (f32[1,2,2,8,64]{2,4,3,1,0:T(8,128)}, f32[1,2,2,8,64]{2,4,3,1,0:T(8,128)}, f32[1,2,2,8,64]{2,4,3,1,0:T(8,128)}, f32[1,2,2,8,64]{2,4,3...) fusion(f32[2,128,8,64]{1,3,2,0:T(8,128)S(1)} %bitcast.359), kind=kLoop, calls=%fused_computation.138 | loop fusion | bytes 311296 | tf_op jit(solution)/shard_map/stack | solution.py:193
  11.0 6.4 %slice_bitcast_fusion.19 = (f32[1,2,2,8,64]{2,4,3,1,0:T(8,128)}, f32[1,2,2,8,64]{2,4,3,1,0:T(8,128)}, f32[1,2,2,8,64]{2,4,3,1,0:T(8,128)}, f32[1,2,2,8,64]{2,4,3...) fusion(f32[2,128,8,64]{1,3,2,0:T(8,128)S(1)} %bitcast.360), kind=kLoop, calls=%fused_computation.119 | loop fusion | bytes 311296 | tf_op jit(solution)/shard_map/stack | solution.py:193
  17.4 6.3 %slice_bitcast_fusion = (f32[1,2,2,8,64]{2,4,3,1,0:T(8,128)}, f32[1,2,2,8,64]{2,4,3,1,0:T(8,128)}, f32[1,2,2,8,64]{2,4,3,1,0:T(8,128)}, f32[1,2,2,8,64]{2,4,3,1,...) fusion(f32[2,128,8,64]{1,3,2,0:T(8,128)S(1)} %bitcast.361), kind=kLoop, calls=%fused_computation.100 | loop fusion | bytes 311296 | tf_op jit(solution)/shard_map/stack | solution.py:193
  23.7 1.2 copy.243
  25.6 1.8 copy.244
  27.4 0.8 copy.245
  28.2 0.8 copy.246
  29.1 0.8 copy.247
  30.7 0.8 copy.249
  31.5 0.8 copy.250
  33.1 0.8 copy.252
  33.9 0.8 copy.253
  34.8 0.8 copy.254
  35.6 0.8 copy.255
  36.4 0.8 copy.256
  38.0 0.8 copy.258
  38.8 0.8 copy.259
  39.6 0.8 copy.260
  41.3 0.8 copy.262
  42.1 0.8 copy.263
  42.9 0.8 copy.264
  43.7 0.8 copy.265
  44.5 0.8 copy.266
  45.4 0.8 copy.267
  48.6 1.0 copy.271
  49.6 0.8 copy.272
  50.4 0.8 copy.273
  51.2 0.8 copy.274
  52.0 0.8 copy.275
  52.9 0.8 copy.276
  54.5 0.8 copy.278
  55.3 0.8 copy.279
  96.4 1.4 reshape.2620
  97.8 11.7 %all-to-all-start = ((f32[64,1,2048]{2,1,0:T(1,128)}), f32[64,1,2048]{2,1,0:T(1,128)S(1)}, u32[]{:S(2)}, u32[]{:S(2)}) async-start(f32[64,1,2048]{2,1,0:T(1,128)} %reshape.2620), calls=%async_computation | async-start | bytes 1048576 | tf_op jit(solution)/shard_map/all_to_all | solution.py:193
  113.9 8.9 %all-to-all-done = f32[64,1,2048]{2,1,0:T(1,128)S(1)} async-done(((f32[64,1,2048]{2,1,0:T(1,128)}), f32[64,1,2048]{2,1,0:T(1,128)S(1)}, u32[]{:S(2)}, u32[]{:S(2)}) %all-to-all-start) | async-done | bytes 524320 | tf_op jit(solution)/shard_map/all_to_all | solution.py:193
  123.2 1.9 reduce.3
  126.3 47.7 %while.16 = (s32[]{:T(128)}, f32[2,128,64]{1,2,0:T(8,128)S(1)}, f32[2,128,64]{1,2,0:T(8,128)S(1)}, f32[8,2,8,8,64]{4,3,0,2,1:T(8,128)S(1)}, s32[8]{0:T(128)S(1)}...) while((s32[]{:T(128)}, f32[2,128,64]{1,2,0:T(8,128)S(1)}, ...), condition=%wide.region_5.6_spmd.clone.clone, body=%wide.region_2.5_spmd.clone.clone.sunk | while | flops 13465411 | bytes 3031079 | solution.py:158
  127.5 4.5 %conditional.4 = (f32[2,128,64]{1,2,0:T(8,128)S(1)}, f32[2,128,64]{1,2,0:T(8,128)S(1)}, f32[1,2,8,8,64]{2,3,4,1,0:T(8,128)S(1)}) conditional(s32[]{:T(128)} %convert_element_type.314, (f32[2,128,64]{1,2,0:T(8,128)S(1)}, f32[2,128,64]{1,2,0:T(8,128)S(1)}) %tuple.202, (s32[]{:T(128)}, s32[2]{0:T(128)S(1)}, s32[2,1,1]{0,2,1:T(1,128)S(1)}, ...), branch_computations={%region_3.3_spmd, %region_4.4_spmd.clone} | conditional | flops 13465407 | bytes 2832748 | solution.py:153
  130.2 0.8 stack.327
  131.1 1.0 convolution_bitcast_fusion
  133.5 4.5 %conditional.4 = (f32[2,128,64]{1,2,0:T(8,128)S(1)}, f32[2,128,64]{1,2,0:T(8,128)S(1)}, f32[1,2,8,8,64]{2,3,4,1,0:T(8,128)S(1)}) conditional(s32[]{:T(128)} %convert_element_type.314, (f32[2,128,64]{1,2,0:T(8,128)S(1)}, f32[2,128,64]{1,2,0:T(8,128)S(1)}) %tuple.202, (s32[]{:T(128)}, s32[2]{0:T(128)S(1)}, s32[2,1,1]{0,2,1:T(1,128)S(1)}, ...), branch_computations={%region_3.3_spmd, %region_4.4_spmd.clone} | conditional | flops 13465407 | bytes 2832748 | solution.py:153
  136.2 0.8 stack.327
  137.0 1.0 convolution_bitcast_fusion
  139.5 4.5 %conditional.4 = (f32[2,128,64]{1,2,0:T(8,128)S(1)}, f32[2,128,64]{1,2,0:T(8,128)S(1)}, f32[1,2,8,8,64]{2,3,4,1,0:T(8,128)S(1)}) conditional(s32[]{:T(128)} %convert_element_type.314, (f32[2,128,64]{1,2,0:T(8,128)S(1)}, f32[2,128,64]{1,2,0:T(8,128)S(1)}) %tuple.202, (s32[]{:T(128)}, s32[2]{0:T(128)S(1)}, s32[2,1,1]{0,2,1:T(1,128)S(1)}, ...), branch_computations={%region_3.3_spmd, %region_4.4_spmd.clone} | conditional | flops 13465407 | bytes 2832748 | solution.py:153
  142.2 0.8 stack.327
  143.0 1.0 convolution_bitcast_fusion
  145.4 4.5 %conditional.4 = (f32[2,128,64]{1,2,0:T(8,128)S(1)}, f32[2,128,64]{1,2,0:T(8,128)S(1)}, f32[1,2,8,8,64]{2,3,4,1,0:T(8,128)S(1)}) conditional(s32[]{:T(128)} %convert_element_type.314, (f32[2,128,64]{1,2,0:T(8,128)S(1)}, f32[2,128,64]{1,2,0:T(8,128)S(1)}) %tuple.202, (s32[]{:T(128)}, s32[2]{0:T(128)S(1)}, s32[2,1,1]{0,2,1:T(1,128)S(1)}, ...), branch_computations={%region_3.3_spmd, %region_4.4_spmd.clone} | conditional | flops 13465407 | bytes 2832748 | solution.py:153
  148.1 0.8 stack.327
  149.0 1.0 convolution_bitcast_fusion
  151.4 4.5 %conditional.4 = (f32[2,128,64]{1,2,0:T(8,128)S(1)}, f32[2,128,64]{1,2,0:T(8,128)S(1)}, f32[1,2,8,8,64]{2,3,4,1,0:T(8,128)S(1)}) conditional(s32[]{:T(128)} %convert_element_type.314, (f32[2,128,64]{1,2,0:T(8,128)S(1)}, f32[2,128,64]{1,2,0:T(8,128)S(1)}) %tuple.202, (s32[]{:T(128)}, s32[2]{0:T(128)S(1)}, s32[2,1,1]{0,2,1:T(1,128)S(1)}, ...), branch_computations={%region_3.3_spmd, %region_4.4_spmd.clone} | conditional | flops 13465407 | bytes 2832748 | solution.py:153
  154.1 0.8 stack.327
  154.9 1.0 convolution_bitcast_fusion
  157.4 4.5 %conditional.4 = (f32[2,128,64]{1,2,0:T(8,128)S(1)}, f32[2,128,64]{1,2,0:T(8,128)S(1)}, f32[1,2,8,8,64]{2,3,4,1,0:T(8,128)S(1)}) conditional(s32[]{:T(128)} %convert_element_type.314, (f32[2,128,64]{1,2,0:T(8,128)S(1)}, f32[2,128,64]{1,2,0:T(8,128)S(1)}) %tuple.202, (s32[]{:T(128)}, s32[2]{0:T(128)S(1)}, s32[2,1,1]{0,2,1:T(1,128)S(1)}, ...), branch_computations={%region_3.3_spmd, %region_4.4_spmd.clone} | conditional | flops 13465407 | bytes 2832748 | solution.py:153
  160.1 0.8 stack.327
  160.9 1.0 convolution_bitcast_fusion
  163.3 4.5 %conditional.4 = (f32[2,128,64]{1,2,0:T(8,128)S(1)}, f32[2,128,64]{1,2,0:T(8,128)S(1)}, f32[1,2,8,8,64]{2,3,4,1,0:T(8,128)S(1)}) conditional(s32[]{:T(128)} %convert_element_type.314, (f32[2,128,64]{1,2,0:T(8,128)S(1)}, f32[2,128,64]{1,2,0:T(8,128)S(1)}) %tuple.202, (s32[]{:T(128)}, s32[2]{0:T(128)S(1)}, s32[2,1,1]{0,2,1:T(1,128)S(1)}, ...), branch_computations={%region_3.3_spmd, %region_4.4_spmd.clone} | conditional | flops 13465407 | bytes 2832748 | solution.py:153
  166.0 0.8 stack.327
  166.9 1.0 convolution_bitcast_fusion
  169.3 4.5 %conditional.4 = (f32[2,128,64]{1,2,0:T(8,128)S(1)}, f32[2,128,64]{1,2,0:T(8,128)S(1)}, f32[1,2,8,8,64]{2,3,4,1,0:T(8,128)S(1)}) conditional(s32[]{:T(128)} %convert_element_type.314, (f32[2,128,64]{1,2,0:T(8,128)S(1)}, f32[2,128,64]{1,2,0:T(8,128)S(1)}) %tuple.202, (s32[]{:T(128)}, s32[2]{0:T(128)S(1)}, s32[2,1,1]{0,2,1:T(1,128)S(1)}, ...), branch_computations={%region_3.3_spmd, %region_4.4_spmd.clone} | conditional | flops 13465407 | bytes 2832748 | solution.py:153
  172.0 0.8 stack.327
  172.8 1.0 convolution_bitcast_fusion
  175.4 15.4 %all_to_all.10 = f32[64,1,256]{2,1,0:T(1,128)S(1)} all-to-all(f32[64,1,256]{2,1,0:T(1,128)S(1)} %reshape.2622), channel_id=1, replica_groups=mesh['beta'=64,'grp'=2] {'beta'}, dimensions={0} | all-to-all | bytes 131072 | tf_op jit(solution)/shard_map/all_to_all | solution.py:17
  192.4 0.8 pad_maximum_fusion
  (579 shorter events, 76.6 us)
Async XLA Ops:
  0.6 1.0 copy-start
  29.9 1.6 copy-start.57
  30.7 1.6 copy-start.56
  31.5 1.6 copy-start.55
  32.3 1.6 copy-start.54
  33.1 1.6 copy-start.53
  33.9 1.6 copy-start.52
  34.7 1.6 copy-start.51
  35.6 1.6 copy-start.50
  36.4 1.6 copy-start.49
  37.2 1.6 copy-start.48
  38.0 1.6 copy-start.47
  38.8 1.6 copy-start.46
  39.6 1.6 copy-start.45
  40.5 1.6 copy-start.44
  41.3 1.6 copy-start.43
  42.1 1.6 copy-start.42
  42.9 1.6 copy-start.41
  43.7 1.6 copy-start.40
  44.5 1.6 copy-start.39
  45.4 1.6 copy-start.38
  46.2 1.6 copy-start.37
  47.0 1.6 copy-start.36
  47.8 1.8 copy-start.35
  48.6 1.8 copy-start.34
  49.6 1.6 copy-start.33
  50.4 1.6 copy-start.32
  51.2 1.6 copy-start.31
  52.0 1.6 copy-start.30
  52.9 1.6 copy-start.29
  53.7 1.6 copy-start.28
  54.5 1.6 copy-start.27
  55.3 1.1 copy-start.26
  56.1 1.1 copy-start.25
  56.4 1.1 copy-start.24
  57.2 1.1 copy-start.23
  57.5 1.1 copy-start.22
  58.3 1.1 copy-start.21
  58.5 1.1 copy-start.20
  59.4 1.1 copy-start.19
  59.6 1.1 copy-start.18
  60.4 1.1 copy-start.17
  60.7 1.1 copy-start.16
  61.5 1.1 copy-start.15
  61.8 1.1 copy-start.14
  62.6 1.1 copy-start.13
  62.9 1.1 copy-start.12
  63.7 1.1 copy-start.11
  63.9 1.1 copy-start.10
  64.8 1.1 copy-start.9
  65.0 1.1 copy-start.8
  65.8 1.1 copy-start.7
  66.1 1.1 copy-start.6
  66.9 1.1 copy-start.5
  67.2 1.1 copy-start.4
  68.0 1.1 copy-start.3
  68.3 1.1 copy-start.2
  69.1 1.1 copy-start.1
  69.1 1.4 copy-start.58
  70.2 0.8 copy-start.93
  72.4 0.7 copy-start.91
  73.1 0.7 copy-start.89
  97.8 24.9 %all-to-all-start = ((f32[64,1,2048]{2,1,0:T(1,128)}), f32[64,1,2048]{2,1,0:T(1,128)S(1)}, u32[]{:S(2)}, u32[]{:S(2)}) async-start(f32[64,1,2048]{2,1,0:T(1,128)} %reshape.2620), calls=%async_computation | async-start | bytes 1048576 | tf_op jit(solution)/shard_map/all_to_all | solution.py:193
  174.2 18.2 %collective-permute-start = (f32[1,8,64,64]{3,2,1,0:T(8,128)S(1)}, f32[1,8,64,64]{3,2,1,0:T(8,128)S(1)}, u32[]{:S(2)}, u32[]{:S(2)}) collective-permute-start(f32[1,8,64,64]{3,2,1,0:T(8,128)S(1)} %get-tuple-element.575), channel_id=1, source_target_pairs={{0,64},{2,66},{4,68},{6,70},{8,72},{10,74},{12,76},{14,78},{16,80}... | collective-permute-start | bytes 393224 | tf_op jit(solution)/shard_map/ppermute | solution.py:12
  (35 other events, 24.8 us)
